TPU v7x, 32 devices: a whole 2x2x4 slice. The times are simulated.
32 devices in a mesh: wide: 2 (over x), context: 4 (over z), tensor: 4 (over y, core).
Axes of the slice: x: 2, y: 2, z: 4, core: 2. Of those that a mesh axis runs over, the one named last changes fastest.
Arguments:
- layer_input: bfloat16 [96, 197, 768], P(('wide', 'tensor')), may hold values from -6 to 6
- qkv_weight: bfloat16 [768, 3, 768], P(('wide', 'tensor'), None, 'context'), may hold values from -0.21875 to 0.21875
- proj_weight: bfloat16 [768, 768], P('context', ('wide', 'tensor')), may hold values from -0.875 to 0.875
- norm_gains: bfloat16 [2, 768], P(None, ('wide', 'tensor')), may hold values from 0.5 to 1.5
- norm_biases: bfloat16 [2, 768], P(None, ('wide', 'tensor')), may hold values from -1.796875 to 1.796875
- router_keys: bfloat16 [768, 8], P(('wide', 'tensor')), may hold values from -0.21875 to 0.21875
- up_weight: bfloat16 [8, 768, 3072], P(('wide', 'context'), None, 'tensor'), may hold values from -0.4375 to 0.4375
- down_weight: bfloat16 [8, 3072, 768], P(('wide', 'context'), 'tensor'), may hold values from -0.4375 to 0.4375
- out_cotangent: bfloat16 [96, 197, 768], P(('wide', 'tensor')), may hold values from -6 to 6
Outputs:
- layer_output: bfloat16 [96, 197, 768], P(('wide', 'tensor'))
- rms_stats: float32 [96, 3], P(('wide', 'tensor'))
- input_grad: bfloat16 [96, 197, 768], P(('wide', 'tensor'))
- qkv_grad: float32 [768, 3, 768], P(('wide', 'tensor'), None, 'context')
- proj_grad: float32 [768, 768], P('context', ('wide', 'tensor'))
- gains_grad: float32 [2, 768], P(None, ('wide', 'tensor'))
- biases_grad: float32 [2, 768], P(None, ('wide', 'tensor'))
- router_grad: float32 [768, 8], P(('wide', 'tensor'))
- up_grad: float32 [8, 768, 3072], P(('wide', 'context'), None, 'tensor')
- down_grad: float32 [8, 3072, 768], P(('wide', 'context'), 'tensor')
All inputs are finite; a program needn't handle non-finite values.
Results may differ from a plain program's by a relative error of at most 0.02.
Values may be sent and summed in bfloat16 or wider, within the bound.
A program may use at most 192 MiB of HBM per device.

v0:
```python
import math
import jax
import jax.numpy as jnp
from jax import lax
from jax.sharding import PartitionSpec as P

HEAD_DIM = 64
norm_eps = 1e-06
highest = lax.Precision.HIGHEST
f32 = jnp.float32
bf16 = jnp.bfloat16


def layer_stats(values):
    center = values - jnp.mean(values, axis=-1, keepdims=True)
    spread = lax.rsqrt(jnp.mean(center * center, axis=-1, keepdims=True) + norm_eps)
    return (center * spread, spread)


def norm_back(upstream, scaled, spread):
    return spread * (
        upstream
        - jnp.mean(upstream, axis=-1, keepdims=True)
        - scaled * jnp.mean(upstream * scaled, axis=-1, keepdims=True)
    )


def root_mean(values):
    return jnp.sqrt(jnp.mean(values * values, axis=(1, 2)))


def dot32(spec, a, b, **kw):
    return jnp.einsum(spec, a, b, preferred_element_type=f32, **kw)


def on_device(
    layer_input,
    qkv_weight,
    proj_weight,
    norm_gains,
    norm_biases,
    router_keys,
    up_weight,
    down_weight,
    out_cotangent,
):
    images, length, width = layer_input.shape
    wide_n = lax.axis_size("wide")
    ctx_n = lax.axis_size("context")
    ten_n = lax.axis_size("tensor")
    share = images // ctx_n
    start = lax.axis_index("context") * share
    slots_n = router_keys.shape[1]
    cols = qkv_weight.shape[2]
    rows = qkv_weight.shape[0]
    heads_b = cols // HEAD_DIM
    logit_scale = 1.6 * math.sqrt(width)
    everyone = ("context", "wide", "tensor")
    plane = ("wide", "tensor")
    pack = jnp.concatenate([qkv_weight.reshape(rows, 3 * cols), proj_weight.T], axis=1)
    weights = lax.all_gather(pack, everyone, axis=0, tiled=True).reshape(ctx_n, width, 4 * cols)
    small = jnp.concatenate([norm_gains, norm_biases, router_keys.T], axis=0)
    small = lax.all_gather(small, plane, axis=1, tiled=True).astype(f32)
    gain_vals, bias_vals, router_vals = (small[0:2], small[2:4], small[4:].T)
    qkv_full = weights[:, :, : 3 * cols]
    proj_t = weights[:, :, 3 * cols :]
    x = lax.dynamic_slice_in_dim(layer_input, start, share, 0).astype(f32)
    g = lax.dynamic_slice_in_dim(out_cotangent, start, share, 0)
    hat1, spread1 = layer_stats(x)
    normed1 = (hat1 * gain_vals[0] + bias_vals[0]).astype(bf16)
    qkv = dot32("bld,cdk->cblk", normed1, qkv_full).astype(bf16)
    qkv = qkv.reshape(ctx_n, share, length, 3, heads_b, HEAD_DIM)
    q, k, v = (qkv[:, :, :, 0], qkv[:, :, :, 1], qkv[:, :, :, 2])
    scores = dot32("cbqhd,cbkhd->cbhqk", q, k) * 0.125
    top = jnp.max(scores, axis=-1, keepdims=True)
    exps = jnp.exp(scores - top)
    probs = exps / jnp.sum(exps, axis=-1, keepdims=True)
    probs_low = probs.astype(bf16)
    heads = dot32("cbhqk,cbkhd->cbqhd", probs_low, v).astype(bf16)
    heads = heads.reshape(ctx_n, share, length, cols)
    attention = dot32("cblh,ceh->ble", heads, proj_t)
    residual = x + attention
    hat2, spread2 = layer_stats(residual)
    second = hat2 * gain_vals[1] + bias_vals[1]
    tokens = second.astype(bf16)
    row_scale = lax.rsqrt(jnp.sum(second * second, axis=-1, keepdims=True) + norm_eps)
    unit = second * row_scale
    col_scale = lax.rsqrt(jnp.sum(router_vals * router_vals, axis=0, keepdims=True) + norm_eps)
    keys_unit = router_vals * col_scale
    logits = logit_scale * jnp.einsum("bld,ds->bls", unit, keys_unit, precision=highest)
    dispatch = jax.nn.softmax(logits, axis=1)
    combine = jax.nn.softmax(logits, axis=2)
    dispatch_low = dispatch.astype(bf16)
    combine_low = combine.astype(bf16)
    slots = dot32("bls,bld->sbd", dispatch_low, tokens).astype(bf16)
    dexp = dot32("bls,bld->sbd", combine_low, g).astype(bf16)
    out = jnp.concatenate([slots, dexp], axis=1)
    got = lax.all_to_all(out, ("wide", "context"), split_axis=0, concat_axis=0, tiled=True)
    got = lax.all_gather(got, "tensor", axis=0, tiled=True)
    n = got.shape[0]
    slot_all = got[:, :share].reshape(n * share, width)
    dexp_all = got[:, share:].reshape(n * share, width)
    up, down = (up_weight[0], down_weight[0])
    hidden = dot32("rd,df->rf", slot_all, up)
    active = jax.nn.gelu(hidden).astype(bf16)
    part_out = dot32("rf,fd->rd", active, down)
    active_grad = dot32("rd,fd->rf", dexp_all, down)
    hidden_grad = jax.vjp(jax.nn.gelu, hidden)[1](active_grad)[0].astype(bf16)
    down_grad = dot32("rf,rd->fd", active, dexp_all)[None]
    up_grad = dot32("rd,rf->df", slot_all, hidden_grad)[None]
    part_slot = dot32("rf,df->rd", hidden_grad, up)
    back = jnp.concatenate(
        [part_out.reshape(n, share, width), part_slot.reshape(n, share, width)], axis=1
    ).astype(bf16)
    back = lax.psum_scatter(back, "tensor", scatter_dimension=0, tiled=True)
    back = lax.all_to_all(back, ("wide", "context"), split_axis=0, concat_axis=0, tiled=True)
    expert_out = back[:, :share]
    dslots = back[:, share:]
    mixture = dot32("bls,sbd->bld", combine_low, expert_out)
    result = residual + mixture
    rms = jnp.stack([root_mean(result), root_mean(attention), root_mean(mixture)], axis=-1)
    layer_output = lax.all_gather(result.astype(bf16), "context", axis=0, tiled=True)
    dcomb = dot32("bld,sbd->bls", g, expert_out)
    ddisp = dot32("bld,sbd->bls", tokens, dslots)
    dtokens = dot32("bls,sbd->bld", dispatch_low, dslots)
    dlogits = combine * (dcomb - jnp.sum(combine * dcomb, axis=2, keepdims=True)) + dispatch * (
        ddisp - jnp.sum(dispatch * ddisp, axis=1, keepdims=True)
    )
    dunit = logit_scale * jnp.einsum("bls,ds->bld", dlogits, keys_unit, precision=highest)
    dkeys = logit_scale * jnp.einsum("bld,bls->ds", unit, dlogits, precision=highest)
    drouter = col_scale * (dkeys - keys_unit * jnp.sum(keys_unit * dkeys, axis=0, keepdims=True))
    dsecond = dtokens + row_scale * (dunit - unit * jnp.sum(unit * dunit, axis=-1, keepdims=True))
    dgain2 = jnp.sum(dsecond * hat2, axis=(0, 1))
    dbias2 = jnp.sum(dsecond, axis=(0, 1))
    dresid = g.astype(f32) + norm_back(dsecond * gain_vals[1], hat2, spread2)
    dattn = dresid.astype(bf16)
    dproj = dot32("ble,cblh->ceh", dattn, heads)
    dheads = dot32("ble,ceh->cblh", dattn, proj_t).astype(bf16)
    dheads = dheads.reshape(ctx_n, share, length, heads_b, HEAD_DIM)
    dprobs = dot32("cbqhd,cbkhd->cbhqk", dheads, v)
    dv = dot32("cbhqk,cbqhd->cbkhd", probs_low, dheads)
    ds = (probs * (dprobs - jnp.sum(probs * dprobs, axis=-1, keepdims=True))).astype(bf16)
    dq = dot32("cbhqk,cbkhd->cbqhd", ds, k) * 0.125
    dk = dot32("cbhqk,cbqhd->cbkhd", ds, q) * 0.125
    dqkv = jnp.stack([dq, dk, dv], axis=3).astype(bf16).reshape(ctx_n, share, length, 3 * cols)
    dqkv_w = dot32("bld,cblk->cdk", normed1, dqkv)
    dnormed1 = dot32("cblk,cdk->bld", dqkv, qkv_full)
    dgain1 = jnp.sum(dnormed1 * hat1, axis=(0, 1))
    dbias1 = jnp.sum(dnormed1, axis=(0, 1))
    dx = (dresid + norm_back(dnormed1 * gain_vals[0], hat1, spread1)).astype(bf16)
    input_grad = lax.all_gather(dx, "context", axis=0, tiled=True)
    rms = lax.all_gather(rms, "context", axis=0, tiled=True)
    dpack = jnp.concatenate([dqkv_w, dproj], axis=2).reshape(ctx_n * width, 4 * cols)
    dpack = lax.psum_scatter(dpack.astype(bf16), everyone, scatter_dimension=0, tiled=True)
    dpack = dpack.astype(f32)
    dsmall = jnp.concatenate([jnp.stack([dgain1, dgain2, dbias1, dbias2], axis=1), drouter], axis=1)
    dsmall = lax.psum(dsmall, "context")
    dsmall = lax.psum_scatter(dsmall, plane, scatter_dimension=0, tiled=True)
    return (
        layer_output,
        rms,
        input_grad,
        dpack[:, : 3 * cols].reshape(rows, 3, cols),
        dpack[:, 3 * cols :].T,
        dsmall[:, 0:2].T,
        dsmall[:, 2:4].T,
        dsmall[:, 4:],
        up_grad,
        down_grad,
    )


def solution(mesh):
    images = P(("wide", "tensor"), None, None)
    qkv = P(("wide", "tensor"), None, "context")
    proj = P("context", ("wide", "tensor"))
    lane = P(None, ("wide", "tensor"))
    rowed = P(("wide", "tensor"), None)
    up = P(("wide", "context"), None, "tensor")
    down = P(("wide", "context"), "tensor", None)
    return jax.shard_map(
        on_device,
        mesh=mesh,
        in_specs=(images, qkv, proj, lane, lane, rowed, up, down, images),
        out_specs=(images, rowed, images, qkv, proj, lane, lane, rowed, up, down),
        check_vma=False,
    )
```

profile of v0, /device:TPU:0, one launch (start us, length us, event | category | flops | bytes accessed | tf_op | source)
XLA Modules:
  0.0 542.7 jit_solution(13824113739327236245)
XLA Ops:
  10.8 10.6 %all-gather = bf16[8,96,12]{1,2,0:T(8,128)(2,1)S(1)} all-gather(bf16[1,96,12]{1,2,0:T(8,128)(2,1)S(1)} %maximum_bitcast_fusion.1), channel_id=1, replica_groups=mesh['wide'=2,'context'=4,'tensor'=4] {'wide','tensor'}, dimensions={0}, use_global_device_ids=true | all-gather | bytes 20736 | tf_op jit(solution)/shard_map/all_gather | solution.py:63
  24.8 53.0 %all-gather.6.cloned.1.call-done = bf16[3072,768]{1,0:T(8,128)(2,1)} async-done(((bf16[96,768]{1,0:T(8,128)(2,1)}), bf16[3072,768]{1,0:T(8,128)(2,1)}) %all-gather.6.cloned.1.call-update) | async-done | bytes 4718608 | tf_op jit(solution)/shard_map/all_gather | solution.py:61
  77.8 6.6 %convert_bitcast_fusion = bf16[4,3,197,576]{3,2,1,0:T(8,128)(2,1)} fusion(bf16[4,768,768]{2,1,0:T(8,128)(2,1)} %bitcast.228, f32[768]{0:T(1024)S(1)} %get-tuple-element.62, f32[768]{0:T(1024)S(1)} %get-tuple-element.63, f32[3,197]{1,0:T(4,128)S(1)} %add_rsqrt_fusion.2, f32[3,197]{1,0:T(4,128)S(1)} %broadcast_multiply_fusion.5, ...), kind=kOutput, calls=%fused_computation.16 | convolution fusion | flops 2095600896 | bytes 7587964 | tf_op jit(solution)/shard_map/bld,cdk->cblk/dot_general | solution.py:33
  84.4 5.8 %copy.124 = bf16[4,3,197,576]{2,3,1,0:T(8,128)(2,1)} copy(bf16[4,3,197,576]{3,2,1,0:T(8,128)(2,1)} %convert_bitcast_fusion) | data formatting | bytes 5446656 | tf_op jit(solution)/shard_map/convert_element_type | solution.py:71
  90.2 2.8 fusion.84
  93.0 6.5 %fusion.140 = (f32[4,3,3,197]{3,2,1,0:T(4,128)S(1)}, f32[4,3,3,197,197]{3,4,2,1,0:T(8,128)S(1)}) fusion(f32[4,3,3,197,197]{3,4,2,1,0:T(8,128)S(1)} %fusion.84), kind=kOutput, calls=%fused_computation.195 | output fusion | flops 5588692 | bytes 11205360 | tf_op jit(solution)/shard_map/sub | solution.py:76
  99.5 3.0 fusion.36
  102.6 4.7 fusion.137
  113.2 10.8 %all_to_all.10 = bf16[8,6,768]{2,1,0:T(8,128)(2,1)S(1)} all-to-all(bf16[8,6,768]{2,1,0:T(8,128)(2,1)S(1)} %copy.130), channel_id=1, replica_groups=mesh['wide'=2,'context'=4,'tensor'=4] {'wide','context'}, dimensions={0} | all-to-all | bytes 147456 | tf_op jit(solution)/shard_map/all_to_all | solution.py:98
  124.1 16.1 %all_gather.20 = bf16[32,6,768]{2,0,1:T(8,128)(2,1)S(1)} all-gather(bf16[8,6,768]{2,0,1:T(8,128)(2,1)S(1)} %copy.131), channel_id=1, replica_groups=mesh['wide'=2,'context'=4,'tensor'=4] {'tensor'}, dimensions={0}, use_global_device_ids=true | all-gather | bytes 368640 | tf_op jit(solution)/shard_map/all_gather | solution.py:99
  143.3 2.6 fusion.106
  152.2 16.8 %reduce-scatter.10.cloned.1.call-done = bf16[8,4608]{1,0:T(8,128)(2,1)} async-done(((bf16[32,4608]{1,0:T(8,128)(2,1)}), bf16[8,4608]{1,0:T(8,128)(2,1)}) %reduce-scatter.10.cloned.1.call-update) | async-done | bytes 73744
  169.9 12.6 %all_to_all.11 = bf16[8,6,768]{2,1,0:T(8,128)(2,1)S(1)} all-to-all(bf16[8,6,768]{2,1,0:T(8,128)(2,1)S(1)} %copy.136), channel_id=1, replica_groups=mesh['wide'=2,'context'=4,'tensor'=4] {'wide','context'}, dimensions={0} | all-to-all | bytes 147456 | tf_op jit(solution)/shard_map/all_to_all | solution.py:116
  184.8 2.2 fusion.119
  187.0 2.9 fusion.122
  193.4 11.0 %multiply_reduce_fusion.2 = (f32[768]{0:T(1024)}, f32[3,197]{1,0:T(4,128)S(1)}, f32[3,197]{1,0:T(4,128)S(1)}, f32[768]{0:T(1024)}, f32[3]{0:T(128)}, /*index=5*/...) fusion(f32[3,197,768]{2,1,0:T(8,128)S(1)} %get-tuple-element.65, f32[3,197]{1,0:T(4,128)S(1)} %copy-done.18, ...), kind=kOutput, calls=%fused_computation.44 | output fusion | flops 13615274 | bytes 10009668 | tf_op jit(solution)/shard_map/mul | solution.py:132
  206.5 4.0 convolution_convert_fusion
  210.6 5.2 multiply_reduce_fusion
  215.8 4.8 multiply_convert_fusion
  222.8 2.7 fusion.48
  228.4 7.0 %fusion.24 = (f32[768]{0:T(1024)S(1)}, f32[3,197]{1,0:T(4,128)S(1)}, f32[3,197]{1,0:T(4,128)S(1)}, f32[768]{0:T(1024)S(1)}, f32[3,197,768,1]{2,1,0,3:T(8,128)}) fusion(f32[3,197]{1,0:T(4,128)S(1)} %copy-done.26, f32[3,197]{1,0:T(4,128)S(1)} %copy-done.16, bf16[12,197,768]{2,1,0:T(8,128)(2,1)} %param.9, s32[]{:T(128)S(6)} %select_n.4, ...), kind=kOutput, calls=%fused_computation.38 | convolution fusion | flops 2096051968 | bytes 10217596 | tf_op jit(solution)/shard_map/cblk,cdk->bld/dot_general | solution.py:33
  236.8 3.3 fusion.23
  240.8 2.6 fusion.49
  243.4 5.1 fusion.8
  248.4 2.5 pad_maximum_fusion
  250.9 6.6 %copy.147 = bf16[4,768,768]{2,1,0:T(8,128)(2,1)} copy(bf16[4,768,768]{1,2,0:T(8,128)(2,1)} %pad_maximum_fusion) | data formatting | bytes 9437184 | tf_op jit(solution)/shard_map/concatenate | solution.py:153
  262.4 11.9 %all-gather.1 = f32[4,3,3]{2,1,0:T(4,128)S(1)} all-gather(f32[1,3,3]{2,1,0:T(4,128)S(1)} %bitcast.226), channel_id=1, replica_groups=mesh['wide'=2,'context'=4,'tensor'=4] {'context'}, dimensions={0}, use_global_device_ids=true | all-gather | bytes 180 | tf_op jit(solution)/shard_map/all_gather | solution.py:152
  276.0 9.0 %psum.8 = f32[96,12]{0,1:T(8,128)S(1)} all-reduce(f32[96,12]{0,1:T(8,128)S(1)} %copy.164), channel_id=1, replica_groups=mesh['wide'=2,'context'=4,'tensor'=4] {'context'}, use_global_device_ids=true, to_apply=%region_30.0 | all-reduce | flops 1152 | bytes 9216 | tf_op jit(solution)/shard_map/psum | solution.py:157
  286.1 55.5 %all-gather.10.cloned.1.call-done = bf16[12,197,768]{2,1,0:T(8,128)(2,1)} async-done(((bf16[3,197,768]{2,1,0:T(8,128)(2,1)}), bf16[12,197,768]{2,1,0:T(8,128)(2,1)}) %all-gather.10.cloned.1.call-update) | async-done | bytes 3631120 | tf_op jit(solution)/shard_map/all_gather | solution.py:151
  341.6 72.3 %all-gather.8.cloned.1.call-done = bf16[12,197,768]{2,1,0:T(8,128)(2,1)} async-done(((bf16[3,197,768]{2,1,0:T(8,128)(2,1)}), bf16[12,197,768]{2,1,0:T(8,128)(2,1)}) %all-gather.8.cloned.1.call-update) | async-done | bytes 3631120 | tf_op jit(solution)/shard_map/all_gather | solution.py:122
  414.0 111.4 %reduce-scatter.8.cloned.1.call-done = bf16[96,768]{1,0:T(8,128)(2,1)} async-done(((bf16[3072,768]{1,0:T(8,128)(2,1)}), bf16[96,768]{1,0:T(8,128)(2,1)}) %reduce-scatter.8.cloned.1.call-update) | async-done | bytes 147472 | tf_op jit(solution)/shard_map/reduce_scatter | solution.py:154
  529.1 4.3 copy.192
  (187 shorter events, 51.1 us)
Async XLA Ops:
  7.2 135.8 %copy-start = (bf16[1,768,768]{2,1,0:T(8,128)(2,1)S(1)}, bf16[1,768,768]{2,1,0:T(8,128)(2,1)}, u32[]{:S(2)}) copy-start(bf16[1,768,768]{2,1,0:T(8,128)(2,1)} %param.15) | copy-start | bytes 3538948
  7.2 70.6 %all-gather.6.cloned.1.call-start = ((), (), s32[]{:S(2)}) async-start(), calls=%async_computation.5 | async-start | bytes 4866048 | tf_op jit(solution)/shard_map/all_gather | solution.py:61
  10.1 159.0 %reduce-scatter.10.cloned.1.call-start = ((), (), s32[]{:S(2)}) async-start(), calls=%async_computation.9 | async-start | bytes 368640
  23.1 61.3 %copy-start.21 = (f32[768]{0:T(1024)}, f32[768]{0:T(1024)S(1)}, u32[]{:S(2)}) copy-start(f32[768]{0:T(1024)S(1)} %get-tuple-element.63) | copy-start | bytes 9220
  23.1 61.3 %copy-start.30 = (f32[768]{0:T(1024)}, f32[768]{0:T(1024)S(1)}, u32[]{:S(2)}) copy-start(f32[768]{0:T(1024)S(1)} %get-tuple-element.62) | copy-start | bytes 9220
  23.1 88.1 %copy-start.23 = (f32[768]{0:T(1024)}, f32[768]{0:T(1024)S(1)}, u32[]{:S(2)}) copy-start(f32[768]{0:T(1024)S(1)} %get-tuple-element.61) | copy-start | bytes 9220
  23.1 61.3 %copy-start.15 = (f32[3,197]{1,0:T(4,128)}, f32[3,197]{1,0:T(4,128)S(1)}, u32[]{:S(2)}) copy-start(f32[3,197]{1,0:T(4,128)S(1)} %broadcast_multiply_fusion.5) | copy-start | bytes 7096
  24.8 83.5 %copy-start.27 = (f32[8]{0:T(128)}, f32[8]{0:T(128)S(1)}, u32[]{:S(2)}) copy-start(f32[8]{0:T(128)S(1)} %add_rsqrt_fusion.3) | copy-start | bytes 100
  24.8 59.6 %copy-start.25 = (f32[3,197]{1,0:T(4,128)}, f32[3,197]{1,0:T(4,128)S(1)}, u32[]{:S(2)}) copy-start(f32[3,197]{1,0:T(4,128)S(1)} %add_rsqrt_fusion.2) | copy-start | bytes 7096
  102.6 4.8 copy-start.39
  151.3 32.8 %copy-start.14 = (f32[3,197,8]{1,2,0:T(8,128)S(1)}, f32[3,197,8]{1,2,0:T(8,128)}, u32[]{:S(2)}) copy-start(f32[3,197,8]{1,2,0:T(8,128)} %get-tuple-element.79) | copy-start | bytes 56740
  151.4 32.8 %copy-start.18 = (f32[3,197]{1,0:T(4,128)S(1)}, f32[3,197]{1,0:T(4,128)}, u32[]{:S(2)}) copy-start(f32[3,197]{1,0:T(4,128)} %copy-done.17) | copy-start | bytes 7096
  151.4 32.8 %copy-start.20 = (f32[3,8]{1,0:T(4,128)S(1)}, f32[3,8]{1,0:T(4,128)}, u32[]{:S(2)}) copy-start(f32[3,8]{1,0:T(4,128)} %copy-done.19) | copy-start | bytes 292
  151.4 32.8 %copy-start.24 = (f32[768]{0:T(1024)S(1)}, f32[768]{0:T(1024)}, u32[]{:S(2)}) copy-start(f32[768]{0:T(1024)} %copy-done.23) | copy-start | bytes 9220
  152.2 122.9 %reduce-scatter.12.cloned.1.call-start = ((), (), s32[]{:S(2)}) async-start(), calls=%async_computation.10 | async-start | bytes 442368
  204.4 6.1 %slice-start = ((s8[7372800]{0:T(1024)(128)(4,1)}), s8[4194304]{0:T(1024)(128)(4,1)S(1)}, s32[]{:S(2)}) async-start(s8[7372800]{0:T(1024)(128)(4,1)} %bitcast.205), calls=%async_computation.11 | async-start | bytes 8388608
  206.4 4.1 copy-start.4
  206.4 4.1 slice-start.1
  206.4 4.2 copy-start.3
  206.5 4.1 copy-start.13
  210.5 5.3 copy-start.40
  222.8 5.4 %slice-start.2 = ((s8[4718592]{0:T(1024)(128)(4,1)}), s8[4194304]{0:T(1024)(128)(4,1)S(1)}, s32[]{:S(2)}) async-start(s8[4718592]{0:T(1024)(128)(4,1)} %bitcast.231), calls=%async_computation.13 | async-start | bytes 8388608
  228.2 7.3 %copy-start.7 = (bf16[4,3,197,3,3,64]{2,5,4,3,1,0:T(8,128)(2,1)}, bf16[4,3,197,3,3,64]{2,5,4,3,1,0:T(8,128)(2,1)S(1)}, u32[]{:S(2)}) copy-start(bf16[4,3,197,3,3,64]{2,5,4,3,1,0:T(8,128)(2,1)S(1)} %copy.144) | copy-start | bytes 8169988
  228.4 7.1 %copy-start.33 = (f32[768]{0:T(1024)S(1)}, f32[768]{0:T(1024)}, u32[]{:S(2)}) copy-start(f32[768]{0:T(1024)} %get-tuple-element.52) | copy-start | bytes 9220
  228.4 7.1 %copy-start.32 = (f32[768]{0:T(1024)S(1)}, f32[768]{0:T(1024)}, u32[]{:S(2)}) copy-start(f32[768]{0:T(1024)} %get-tuple-element.56) | copy-start | bytes 9220
  228.4 7.1 %copy-start.29 = (f32[8]{0:T(128)S(1)}, f32[8]{0:T(128)}, u32[]{:S(2)}) copy-start(f32[8]{0:T(128)} %copy-done.27) | copy-start | bytes 100
  228.4 7.1 %copy-start.36 = (f32[8]{0:T(128)S(1)}, f32[8]{0:T(128)}, u32[]{:S(2)}) copy-start(f32[8]{0:T(128)} %get-tuple-element.90) | copy-start | bytes 100
  228.4 8.4 %copy-start.5 = (f32[3,197,768]{2,1,0:T(8,128)S(1)}, f32[3,197,768]{2,1,0:T(8,128)}, u32[]{:S(2)}) copy-start(f32[3,197,768]{2,1,0:T(8,128)} %copy-done.4) | copy-start | bytes 5446660
  236.7 104.9 %all-gather.10.cloned.1.call-start = ((), (), s32[]{:S(2)}) async-start(), calls=%async_computation.7 | async-start | bytes 4608000 | tf_op jit(solution)/shard_map/all_gather | solution.py:151
  240.1 173.8 %all-gather.8.cloned.1.call-start = ((), (), s32[]{:S(2)}) async-start(), calls=%async_computation.6 | async-start | bytes 4608000 | tf_op jit(solution)/shard_map/all_gather | solution.py:122
  240.7 284.6 %reduce-scatter.8.cloned.1.call-start = ((), (), s32[]{:S(2)}) async-start(), calls=%async_computation.8 | async-start | bytes 4866048 | tf_op jit(solution)/shard_map/reduce_scatter | solution.py:154
  529.1 4.3 copy-start.6
  (21 other events, 41.7 us)
Sparse Core Ops, SparseCore 0:
  11.5 66.2 all-gather.5
  152.3 16.6 reduce-scatter.9
  236.8 30.2 reduce-scatter.11
  269.1 72.4 all-gather.9
  343.0 70.8 all-gather.7
  419.3 106.0 reduce-scatter.7
where the time goes:
time: 552 us; the launch traced here: 543 us
  waiting for transfers between devices  310 us (56%)
  matrix products  72.2 us (13%)
  blocking collectives  71 us (13%)
  other arithmetic  38.7 us (7%)
  local copies, waits for them, and re-layouts  35.6 us (6%)
  between operations  15.3 us (3%)
    reduce_scatter x1, waiting for transfers between devices, on_device(): lax.psum_scatter(dpack.astype(bf16), everyone, scatter_dimension=0, tiled...  111 us
    all_gather x1, waiting for transfers between devices, on_device(): lax.all_gather(result.astype(bf16), 'context', axis=0, tiled=True)  72.3 us
    dot_general x24, matrix products, dot32(): return jnp.einsum(spec, a, b, preferred_element_type=f32, **kw)  65.1 us
    all_gather x1, waiting for transfers between devices, on_device(): input_grad = lax.all_gather(dx, 'context', axis=0, tiled=True)  55.5 us
    all_gather x1, waiting for transfers between devices, on_device(): lax.all_gather(pack, everyone, axis=0, tiled=True)  53 us
    unnamed x8, waiting for transfers between devices  17.4 us
    all_gather x1, blocking collectives, on_device(): got = lax.all_gather(got, 'tensor', axis=0, tiled=True)  16.1 us
    unnamed x103, local copies, waits for them, and re-layouts  13.7 us
  transfers between devices with their start and end apart: 6, of which 5 were waited for; matrix products, arithmetic and copies ran while one was open for 6% of the time, Pallas kernels for 0%

commit v1 on v0

--- a/solution.py
+++ b/solution.py
@@ -9,6 +9,34 @@
 highest = lax.Precision.HIGHEST
 f32 = jnp.float32
 bf16 = jnp.bfloat16
+
+
+def squares_write(field, axis_no, xx):
+    mid_arr = field.shape
+    v1 = field.reshape(*mid_arr[:axis_no], xx, mid_arr[axis_no] // xx, *mid_arr[axis_no + 1 :])
+    return jnp.moveaxis(v1, axis_no, 0)
+
+
+def pass_the_table(a0, dim_k):
+    r2 = list(a0.shape[1:])
+    r2[dim_k] *= a0.shape[0]
+    return jnp.moveaxis(a0, 0, dim_k).reshape(r2)
+
+
+def begin_the_orders(inner_x, named_axis, vector, z_in):
+    piece_next, u_next = (jax.lax.axis_size(named_axis), jax.lax.axis_index(named_axis))
+    outer = squares_write(inner_x, vector, piece_next)
+    before = outer
+    for j in range(1, piece_next):
+        found_now, block_last = ((u_next + j) % piece_next, (u_next - j) % piece_next)
+        a_now = lax.dynamic_index_in_dim(outer, found_now, 0)
+        met_up = jax.lax.ppermute(
+            a_now,
+            axis_name=named_axis,
+            perm=list(map(lambda m: (m, (m + j) % piece_next), range(piece_next))),
+        )
+        before = lax.dynamic_update_slice_in_dim(before, met_up, block_last, axis=0)
+    return pass_the_table(before, z_in)
 
 
 def layer_stats(values):
@@ -113,7 +141,7 @@
         [part_out.reshape(n, share, width), part_slot.reshape(n, share, width)], axis=1
     ).astype(bf16)
     back = lax.psum_scatter(back, "tensor", scatter_dimension=0, tiled=True)
-    back = lax.all_to_all(back, ("wide", "context"), split_axis=0, concat_axis=0, tiled=True)
+    back = begin_the_orders(back, ("wide", "context"), 0, 0)
     expert_out = back[:, :share]
     dslots = back[:, share:]
     mixture = dot32("bls,sbd->bld", combine_low, expert_out)

time: 552 us -> 561 us (1.016)
  blocking collectives: 71 us -> 50.9 us
  starting transfers between devices: 0.24 us -> 12.6 us
  local copies, waits for them, and re-layouts: 35.6 us -> 47.2 us
  matrix products: 72.2 us -> 78.6 us
    all_to_all x1 -> x0, blocking collectives: 12.6 us -> none  [on_device(): lax.all_to_all(back, ('wide', 'context'), split_axis=0, concat_axis=0, ti...]
    ppermute x0 -> x7, starting transfers between devices: none -> 12.2 us  [begin_the_orders(): jax.lax.ppermute(a_now, axis_name=named_axis, perm=list(map(lambda m: (m,...]
    dynamic_update_slice x0 -> x7, local copies, waits for them, and re-layouts: none -> 11 us  [begin_the_orders(): before = lax.dynamic_update_slice_in_dim(before, met_up, block_last, axis=0)]
    all_gather x1, blocking collectives: 16.1 us -> 6.33 us  [on_device(): got = lax.all_gather(got, 'tensor', axis=0, tiled=True)]
    dot_general x24, matrix products: 65.1 us -> 70.9 us  [dot32(): return jnp.einsum(spec, a, b, preferred_element_type=f32, **kw)]
    unnamed x103 -> x116, local copies, waits for them, and re-layouts: 13.7 us -> 13.8 us
  transfers between devices with their start and end apart: 6 -> 13, of which waited for: 5 -> 8; matrix products, arithmetic and copies ran while one was open for 6% -> 6% of each run, Pallas kernels for 0% -> 0%
where the time goes in v1:
time: 561 us; the launch traced here: 551 us
  waiting for transfers between devices  312 us (56%)
  matrix products  78.6 us (14%)
  blocking collectives  50.9 us (9%)
  local copies, waits for them, and re-layouts  47.2 us (8%)
  other arithmetic  34.7 us (6%)
  between operations  15.3 us (3%)
  starting transfers between devices  12.6 us (2%)
    reduce_scatter x1, waiting for transfers between devices, on_device(): lax.psum_scatter(dpack.astype(bf16), everyone, scatter_dimension=0, tiled...  111 us
    all_gather x1, waiting for transfers between devices, on_device(): lax.all_gather(result.astype(bf16), 'context', axis=0, tiled=True)  72.4 us
    dot_general x24, matrix products, dot32(): return jnp.einsum(spec, a, b, preferred_element_type=f32, **kw)  70.9 us
    all_gather x1, waiting for transfers between devices, on_device(): input_grad = lax.all_gather(dx, 'context', axis=0, tiled=True)  56.4 us
    all_gather x1, waiting for transfers between devices, on_device(): lax.all_gather(pack, everyone, axis=0, tiled=True)  53 us
    unnamed x8, waiting for transfers between devices  17.3 us
    unnamed x116, local copies, waits for them, and re-layouts  13.8 us
    ppermute x7, starting transfers between devices, begin_the_orders(): jax.lax.ppermute(a_now, axis_name=named_axis, perm=list(map(lambda m: (m,...  12.2 us
  transfers between devices with their start and end apart: 13, of which 8 were waited for; matrix products, arithmetic and copies ran while one was open for 6% of the time, Pallas kernels for 0%

profile of v1, /device:TPU:0, one launch (start us, length us, event | category | flops | bytes accessed | tf_op | source)
XLA Modules:
  0.0 551.5 jit_solution(7027963614523241768)
XLA Ops:
  10.8 10.6 %all-gather = bf16[8,96,12]{1,2,0:T(8,128)(2,1)S(1)} all-gather(bf16[1,96,12]{1,2,0:T(8,128)(2,1)S(1)} %maximum_bitcast_fusion.1), channel_id=1, replica_groups=mesh['wide'=2,'context'=4,'tensor'=4] {'wide','tensor'}, dimensions={0}, use_global_device_ids=true | all-gather | bytes 20736 | tf_op jit(solution)/shard_map/all_gather | solution.py:91
  24.8 53.0 %all-gather.6.cloned.1.call-done = bf16[3072,768]{1,0:T(8,128)(2,1)} async-done(((bf16[96,768]{1,0:T(8,128)(2,1)}), bf16[3072,768]{1,0:T(8,128)(2,1)}) %all-gather.6.cloned.1.call-update) | async-done | bytes 4718608 | tf_op jit(solution)/shard_map/all_gather | solution.py:89
  77.8 6.6 %convert_bitcast_fusion = bf16[4,3,197,576]{3,2,1,0:T(8,128)(2,1)} fusion(bf16[4,768,768]{2,1,0:T(8,128)(2,1)} %bitcast.271, f32[768]{0:T(1024)S(1)} %get-tuple-element.62, f32[768]{0:T(1024)S(1)} %get-tuple-element.63, f32[3,197]{1,0:T(4,128)S(1)} %add_rsqrt_fusion.2, f32[3,197]{1,0:T(4,128)S(1)} %broadcast_multiply_fusion.5, ...), kind=kOutput, calls=%fused_computation.16 | convolution fusion | flops 2095600896 | bytes 7587964 | tf_op jit(solution)/shard_map/bld,cdk->cblk/dot_general | solution.py:61
  84.4 5.8 %copy.153 = bf16[4,3,197,576]{2,3,1,0:T(8,128)(2,1)} copy(bf16[4,3,197,576]{3,2,1,0:T(8,128)(2,1)} %convert_bitcast_fusion) | data formatting | bytes 5446656 | tf_op jit(solution)/shard_map/convert_element_type | solution.py:99
  90.2 2.8 fusion.71
  93.0 6.5 %fusion.125 = (f32[4,3,3,197]{3,2,1,0:T(4,128)S(1)}, f32[4,3,3,197,197]{3,4,2,1,0:T(8,128)S(1)}) fusion(f32[4,3,3,197,197]{3,4,2,1,0:T(8,128)S(1)} %fusion.71), kind=kOutput, calls=%fused_computation.199 | output fusion | flops 5588692 | bytes 11205360 | tf_op jit(solution)/shard_map/sub | solution.py:104
  99.6 3.0 fusion.34
  102.6 4.7 fusion.123
  113.7 10.8 %all_to_all.5 = bf16[8,6,768]{2,1,0:T(8,128)(2,1)S(1)} all-to-all(bf16[8,6,768]{2,1,0:T(8,128)(2,1)S(1)} %copy.159), channel_id=1, replica_groups=mesh['wide'=2,'context'=4,'tensor'=4] {'wide','context'}, dimensions={0} | all-to-all | bytes 147456 | tf_op jit(solution)/shard_map/all_to_all | solution.py:126
  124.6 6.3 %all_gather.20 = bf16[32,6,768]{2,0,1:T(8,128)(2,1)S(1)} all-gather(bf16[8,6,768]{2,0,1:T(8,128)(2,1)S(1)} %copy.160), channel_id=1, replica_groups=mesh['wide'=2,'context'=4,'tensor'=4] {'tensor'}, dimensions={0}, use_global_device_ids=true | all-gather | bytes 368640 | tf_op jit(solution)/shard_map/all_gather | solution.py:127
  134.0 2.6 fusion.87
  143.1 16.7 %reduce-scatter.10.cloned.1.call-done = bf16[8,4608]{1,0:T(8,128)(2,1)} async-done(((bf16[32,4608]{1,0:T(8,128)(2,1)}), bf16[8,4608]{1,0:T(8,128)(2,1)}) %reduce-scatter.10.cloned.1.call-update) | async-done | bytes 73744
  189.1 2.7 fusion.100
  191.9 2.9 fusion.103
  194.8 6.0 %fusion = f32[3,197,768]{2,1,0:T(8,128)} fusion(f32[3,197,768]{2,1,0:T(8,128)} %fusion.103, f32[3,197]{1,0:T(4,128)S(1)} %copy-done.24, f32[768]{0:T(1024)S(1)} %copy-done.18, f32[768]{0:T(1024)S(1)} %get-tuple-element.60, f32[3,197]{1,0:T(4,128)S(1)} %add_rsqrt_fusion.1, f32[3,197,768]{2,1,0:T(8,128)S(1)} %get-tuple-element.65, ...), kind=kOutput, calls=%fused_computation | output fusion | flops 3178574 | bytes 5459892 | tf_op jit(solution)/shard_map/mul | solution.py:160
  200.8 4.4 multiply_add_fusion.1
  205.1 4.2 multiply_reduce_fusion.2
  211.9 4.0 convolution_convert_fusion
  216.0 5.2 multiply_reduce_fusion
  221.2 4.8 multiply_convert_fusion
  228.2 2.7 fusion.43
  233.9 7.0 %fusion.24 = (f32[768]{0:T(1024)S(1)}, f32[3,197]{1,0:T(4,128)S(1)}, f32[3,197]{1,0:T(4,128)S(1)}, f32[768]{0:T(1024)S(1)}, f32[3,197,768,1]{2,1,0,3:T(8,128)}) fusion(f32[3,197]{1,0:T(4,128)S(1)} %copy-done.31, f32[3,197]{1,0:T(4,128)S(1)} %copy-done.22, bf16[12,197,768]{2,1,0:T(8,128)(2,1)} %param.9, s32[]{:T(128)S(6)} %select_n.106, ...), kind=kOutput, calls=%fused_computation.38 | convolution fusion | flops 2096051968 | bytes 10217596 | tf_op jit(solution)/shard_map/cblk,cdk->bld/dot_general | solution.py:61
  242.2 3.3 fusion.23
  246.5 2.5 fusion.44
  249.0 5.1 fusion.8
  256.6 6.6 %copy.187 = bf16[4,768,768]{2,1,0:T(8,128)(2,1)} copy(bf16[4,768,768]{1,2,0:T(8,128)(2,1)} %pad_maximum_fusion) | data formatting | bytes 9437184 | tf_op jit(solution)/shard_map/concatenate | solution.py:181
  268.1 11.9 %all-gather.1 = f32[4,3,3]{2,1,0:T(4,128)S(1)} all-gather(f32[1,3,3]{2,1,0:T(4,128)S(1)} %bitcast.269), channel_id=1, replica_groups=mesh['wide'=2,'context'=4,'tensor'=4] {'context'}, dimensions={0}, use_global_device_ids=true | all-gather | bytes 180 | tf_op jit(solution)/shard_map/all_gather | solution.py:180
  281.6 11.3 %psum.8 = f32[96,12]{0,1:T(8,128)S(1)} all-reduce(f32[96,12]{0,1:T(8,128)S(1)} %copy.204), channel_id=1, replica_groups=mesh['wide'=2,'context'=4,'tensor'=4] {'context'}, use_global_device_ids=true, to_apply=%region_30.31 | all-reduce | flops 1152 | bytes 9216 | tf_op jit(solution)/shard_map/psum | solution.py:185
  294.1 56.4 %all-gather.10.cloned.1.call-done = bf16[12,197,768]{2,1,0:T(8,128)(2,1)} async-done(((bf16[3,197,768]{2,1,0:T(8,128)(2,1)}), bf16[12,197,768]{2,1,0:T(8,128)(2,1)}) %all-gather.10.cloned.1.call-update) | async-done | bytes 3631120 | tf_op jit(solution)/shard_map/all_gather | solution.py:179
  350.5 72.4 %all-gather.8.cloned.1.call-done = bf16[12,197,768]{2,1,0:T(8,128)(2,1)} async-done(((bf16[3,197,768]{2,1,0:T(8,128)(2,1)}), bf16[12,197,768]{2,1,0:T(8,128)(2,1)}) %all-gather.8.cloned.1.call-update) | async-done | bytes 3631120 | tf_op jit(solution)/shard_map/all_gather | solution.py:150
  422.9 111.4 %reduce-scatter.8.cloned.1.call-done = bf16[96,768]{1,0:T(8,128)(2,1)} async-done(((bf16[3072,768]{1,0:T(8,128)(2,1)}), bf16[96,768]{1,0:T(8,128)(2,1)}) %reduce-scatter.8.cloned.1.call-update) | async-done | bytes 147472 | tf_op jit(solution)/shard_map/reduce_scatter | solution.py:182
  538.0 4.3 copy.246
  (226 shorter events, 77.5 us)
Async XLA Ops:
  7.2 126.5 %copy-start = (bf16[1,768,768]{2,1,0:T(8,128)(2,1)S(1)}, bf16[1,768,768]{2,1,0:T(8,128)(2,1)}, u32[]{:S(2)}) copy-start(bf16[1,768,768]{2,1,0:T(8,128)(2,1)} %param.15) | copy-start | bytes 3538948
  7.2 70.6 %all-gather.6.cloned.1.call-start = ((), (), s32[]{:S(2)}) async-start(), calls=%async_computation.4 | async-start | bytes 4866048 | tf_op jit(solution)/shard_map/all_gather | solution.py:89
  10.1 149.7 %reduce-scatter.10.cloned.1.call-start = ((), (), s32[]{:S(2)}) async-start(), calls=%async_computation.8 | async-start | bytes 368640
  23.1 61.3 %copy-start.28 = (f32[768]{0:T(1024)}, f32[768]{0:T(1024)S(1)}, u32[]{:S(2)}) copy-start(f32[768]{0:T(1024)S(1)} %get-tuple-element.63) | copy-start | bytes 9220
  23.1 61.3 %copy-start.35 = (f32[768]{0:T(1024)}, f32[768]{0:T(1024)S(1)}, u32[]{:S(2)}) copy-start(f32[768]{0:T(1024)S(1)} %get-tuple-element.62) | copy-start | bytes 9220
  23.1 88.6 %copy-start.17 = (f32[768]{0:T(1024)}, f32[768]{0:T(1024)S(1)}, u32[]{:S(2)}) copy-start(f32[768]{0:T(1024)S(1)} %get-tuple-element.61) | copy-start | bytes 9220
  23.1 61.3 %copy-start.21 = (f32[3,197]{1,0:T(4,128)}, f32[3,197]{1,0:T(4,128)S(1)}, u32[]{:S(2)}) copy-start(f32[3,197]{1,0:T(4,128)S(1)} %broadcast_multiply_fusion.5) | copy-start | bytes 7096
  24.8 83.5 %copy-start.32 = (f32[8]{0:T(128)}, f32[8]{0:T(128)S(1)}, u32[]{:S(2)}) copy-start(f32[8]{0:T(128)S(1)} %add_rsqrt_fusion.3) | copy-start | bytes 100
  24.8 59.6 %copy-start.30 = (f32[3,197]{1,0:T(4,128)}, f32[3,197]{1,0:T(4,128)S(1)}, u32[]{:S(2)}) copy-start(f32[3,197]{1,0:T(4,128)S(1)} %add_rsqrt_fusion.2) | copy-start | bytes 7096
  140.4 45.6 %copy-start.13 = (f32[3,197,8]{1,2,0:T(8,128)S(1)}, f32[3,197,8]{1,2,0:T(8,128)}, u32[]{:S(2)}) copy-start(f32[3,197,8]{1,2,0:T(8,128)} %get-tuple-element.82) | copy-start | bytes 56740
  140.5 45.6 %copy-start.20 = (f32[3,197]{1,0:T(4,128)S(1)}, f32[3,197]{1,0:T(4,128)}, u32[]{:S(2)}) copy-start(f32[3,197]{1,0:T(4,128)} %copy-done.19) | copy-start | bytes 7096
  142.1 45.5 %copy-start.16 = (f32[3,197,8]{1,2,0:T(8,128)S(1)}, f32[3,197,8]{1,2,0:T(8,128)}, u32[]{:S(2)}) copy-start(f32[3,197,8]{1,2,0:T(8,128)} %get-tuple-element.84) | copy-start | bytes 56740
  142.1 45.5 %copy-start.18 = (f32[768]{0:T(1024)S(1)}, f32[768]{0:T(1024)}, u32[]{:S(2)}) copy-start(f32[768]{0:T(1024)} %copy-done.17) | copy-start | bytes 9220
  142.1 45.5 %copy-start.27 = (f32[3,8]{1,0:T(4,128)S(1)}, f32[3,8]{1,0:T(4,128)}, u32[]{:S(2)}) copy-start(f32[3,8]{1,0:T(4,128)} %copy-done.26) | copy-start | bytes 292
  142.9 137.9 %reduce-scatter.12.cloned.1.call-start = ((), (), s32[]{:S(2)}) async-start(), calls=%async_computation.9 | async-start | bytes 442368
  161.1 8.4 %collective-permute-start = (bf16[1,1,6,768]{3,2,1,0:T(8,128)(2,1)S(1)}, bf16[1,1,6,768]{3,2,1,0:T(8,128)(2,1)S(1)}, u32[]{:S(2)}, u32[]{:S(2)}) collective-permute-start(bf16[1,1,6,768]{3,2,1,0:T(8,128)(2,1)S(1)} %bitcast.268), channel_id=1, source_target_pairs={{0,4},{4,8},{8,12},{12,16},{16,20},{20,24},{24,28},{28,0},{1,5},{5... | collective-permute-start | bytes 27656 | tf_op jit(solution)/shard_map/ppermute | solution.py:33
  162.6 8.3 %collective-permute-start.1 = (bf16[1,1,6,768]{3,2,1,0:T(8,128)(2,1)S(1)}, bf16[1,1,6,768]{3,2,1,0:T(8,128)(2,1)S(1)}, u32[]{:S(2)}, u32[]{:S(2)}) collective-permute-start(bf16[1,1,6,768]{3,2,1,0:T(8,128)(2,1)S(1)} %bitcast.267), channel_id=1, source_target_pairs={{0,8},{4,12},{8,16},{12,20},{16,24},{20,28},{24,0},{28,4},{1,9},{5... | collective-permute-start | bytes 27656 | tf_op jit(solution)/shard_map/ppermute | solution.py:33
  165.0 8.3 %collective-permute-start.2 = (bf16[1,1,6,768]{3,2,1,0:T(8,128)(2,1)S(1)}, bf16[1,1,6,768]{3,2,1,0:T(8,128)(2,1)S(1)}, u32[]{:S(2)}, u32[]{:S(2)}) collective-permute-start(bf16[1,1,6,768]{3,2,1,0:T(8,128)(2,1)S(1)} %bitcast.258), channel_id=1, source_target_pairs={{0,12},{4,16},{8,20},{12,24},{16,28},{20,0},{24,4},{28,8},{1,13},{... | collective-permute-start | bytes 27656 | tf_op jit(solution)/shard_map/ppermute | solution.py:33
  167.4 6.0 %collective-permute-start.3 = (bf16[1,1,6,768]{3,2,1,0:T(8,128)(2,1)S(1)}, bf16[1,1,6,768]{3,2,1,0:T(8,128)(2,1)S(1)}, u32[]{:S(2)}, u32[]{:S(2)}) collective-permute-start(bf16[1,1,6,768]{3,2,1,0:T(8,128)(2,1)S(1)} %bitcast.260), channel_id=1, source_target_pairs={{0,16},{4,20},{8,24},{12,28},{16,0},{20,4},{24,8},{28,12},{1,17},{... | collective-permute-start | bytes 27656 | tf_op jit(solution)/shard_map/ppermute | solution.py:33
  167.9 5.5 collective-permute-start.4
  169.5 4.7 collective-permute-start.5
  170.9 4.1 collective-permute-start.6
  175.0 14.1 %copy-start.24 = (f32[3,197]{1,0:T(4,128)S(1)}, f32[3,197]{1,0:T(4,128)}, u32[]{:S(2)}) copy-start(f32[3,197]{1,0:T(4,128)} %copy-done.23) | copy-start | bytes 7096
  175.0 14.1 %copy-start.33 = (f32[8]{0:T(128)S(1)}, f32[8]{0:T(128)}, u32[]{:S(2)}) copy-start(f32[8]{0:T(128)} %copy-done.32) | copy-start | bytes 100
  233.6 7.3 %copy-start.7 = (bf16[4,3,197,3,3,64]{2,5,4,3,1,0:T(8,128)(2,1)}, bf16[4,3,197,3,3,64]{2,5,4,3,1,0:T(8,128)(2,1)S(1)}, u32[]{:S(2)}) copy-start(bf16[4,3,197,3,3,64]{2,5,4,3,1,0:T(8,128)(2,1)S(1)} %copy.184) | copy-start | bytes 8169988
  233.8 7.1 %copy-start.25 = (f32[768,8]{0,1:T(8,128)S(1)}, f32[768,8]{0,1:T(8,128)}, u32[]{:S(2)}) copy-start(f32[768,8]{0,1:T(8,128)} %get-tuple-element.95) | copy-start | bytes 73732
  233.8 7.1 %copy-start.34 = (f32[8]{0:T(128)S(1)}, f32[8]{0:T(128)}, u32[]{:S(2)}) copy-start(f32[8]{0:T(128)} %copy-done.32) | copy-start | bytes 100
  233.8 7.1 %copy-start.39 = (f32[8]{0:T(128)S(1)}, f32[8]{0:T(128)}, u32[]{:S(2)}) copy-start(f32[8]{0:T(128)} %get-tuple-element.94) | copy-start | bytes 100
  233.8 8.4 %copy-start.5 = (f32[3,197,768]{2,1,0:T(8,128)S(1)}, f32[3,197,768]{2,1,0:T(8,128)}, u32[]{:S(2)}) copy-start(f32[3,197,768]{2,1,0:T(8,128)} %copy-done.4) | copy-start | bytes 5446660
  242.1 108.4 %all-gather.10.cloned.1.call-start = ((), (), s32[]{:S(2)}) async-start(), calls=%async_computation.6 | async-start | bytes 4608000 | tf_op jit(solution)/shard_map/all_gather | solution.py:179
  245.6 177.3 %all-gather.8.cloned.1.call-start = ((), (), s32[]{:S(2)}) async-start(), calls=%async_computation.5 | async-start | bytes 4608000 | tf_op jit(solution)/shard_map/all_gather | solution.py:150
  246.2 288.1 %reduce-scatter.8.cloned.1.call-start = ((), (), s32[]{:S(2)}) async-start(), calls=%async_computation.7 | async-start | bytes 4866048 | tf_op jit(solution)/shard_map/reduce_scatter | solution.py:182
  (31 other events, 97.8 us)
Sparse Core Ops, SparseCore 0:
  11.5 66.2 all-gather.5
  143.0 16.6 reduce-scatter.9
  242.3 34.2 reduce-scatter.11
  278.0 72.4 all-gather.9
  351.9 70.9 all-gather.7
  428.2 106.0 reduce-scatter.7
